TPU v7x, 32 devices: a whole 2x2x4 slice. The times are simulated.
32 devices in a mesh: seq: 8 (over z, y), head: 4 (over x, core).
Axes of the slice: x: 2, y: 2, z: 4, core: 2. Of those that a mesh axis runs over, the one named last changes fastest.
Arguments:
- query: bfloat16 [8, 40, 128], P(None, 'head'), may hold values from -400 to 400
- key_cache: bfloat16 [8, 4096, 8, 128], P(None, 'seq', 'head'), may hold values from -6 to 6
- value_cache: bfloat16 [8, 4096, 8, 128], P(None, 'seq', 'head'), may hold values from -6 to 6
- new_key: bfloat16 [8, 8, 128], P(None, 'head'), may hold values from -6 to 6
- new_value: bfloat16 [8, 8, 128], P(None, 'head'), may hold values from -6 to 6
- lengths: int32 [8], replicated, may hold values from 1024 to 4096, as said below
- out_weight: bfloat16 [5120, 5120], P('head', 'seq'), may hold values from -0.078125 to 0.078125
Outputs:
- projected: float32 [8, 5120], P(None, 'seq')
Inputs may be any that keep to these rules, and one draw needn't show every extreme that they name: `lengths`: some sequence has exactly 4096 cached tokens.
All inputs are finite; a program needn't handle non-finite values.
Results may differ from a plain program's by a relative error of at most 0.0064.
Values sent between devices are 32-bit elements; how exact they have to be, the bound alone decides.
No kernel may reach another device: no remote copies, remote signals or barrier semaphores. Data moves between devices by JAX's collectives and lax.ppermute only.
A program may use at most 64 MiB of HBM per device.

v0:
```python
import math
import jax
import jax.numpy as jnp
from jax import lax
from jax.sharding import PartitionSpec as P

THETA_BASE = 10000000.0
NEG_FILL = -1e30


def apply_rotary(values, positions):
    half_width = values.shape[-1] // 2
    frequency = jnp.exp(
        jnp.arange(half_width, dtype=jnp.float32)
        * jnp.float32(-2.0 * math.log(THETA_BASE) / values.shape[-1])
    )
    angles = positions[..., None] * frequency
    cos_part = jnp.cos(angles)
    sin_part = jnp.sin(angles)
    lower_section = values[..., :half_width]
    upper_half = values[..., half_width:]
    return jnp.concatenate(
        [
            lower_section * cos_part - upper_half * sin_part,
            upper_half * cos_part + lower_section * sin_part,
        ],
        axis=-1,
    )


def query_positions(lengths, stretch_len):
    remainder = lengths % stretch_len
    return jnp.stack(
        [
            remainder,
            remainder + stretch_len,
            jnp.zeros_like(remainder) + (stretch_len + stretch_len // 2),
        ],
        axis=-1,
    ).astype(jnp.float32)


def body(query, key_cache, value_cache, new_key, new_value, lengths, out_weight):
    seq_count = lax.axis_size("seq")
    batch, span_len, kv_local, head_width = key_cache.shape
    heads_local = query.shape[1]
    group_size = heads_local // kv_local
    stretch_len = span_len * seq_count // 8
    scaling = 1.0 / math.sqrt(head_width)
    positions = lax.axis_index("seq") * span_len + jnp.arange(span_len, dtype=jnp.int32)
    query_pos = query_positions(lengths, stretch_len)
    query_rot = apply_rotary(query.astype(jnp.float32)[:, None], query_pos[:, :, None]).astype(
        jnp.bfloat16
    )
    key_rot = apply_rotary(
        key_cache.astype(jnp.float32), (positions % stretch_len).astype(jnp.float32)[None, :, None]
    ).astype(jnp.bfloat16)
    query_by_group = query_rot.reshape(batch, 3, kv_local, group_size, head_width)
    query_stretch = lengths // stretch_len
    key_stretch = positions // stretch_len
    key_class = jnp.where(
        key_stretch[None] == query_stretch[:, None],
        0,
        jnp.where(key_stretch[None] == query_stretch[:, None] - 1, 1, 2),
    )
    block_class = key_class[:, 0][:, None, None, None]
    picked = jnp.where(
        block_class == 0,
        query_by_group[:, 0],
        jnp.where(block_class == 1, query_by_group[:, 1], query_by_group[:, 2]),
    )
    selected_branch = (
        jnp.einsum("bkgd,bpkd->bkgp", picked, key_rot, preferred_element_type=jnp.float32) * scaling
    )
    live_mask = (positions[None] < lengths[:, None])[:, None, None, :]
    masked = jnp.where(live_mask, selected_branch, NEG_FILL)
    block_max = jnp.max(masked, axis=-1)
    weights = jnp.where(live_mask, jnp.exp(masked - block_max[..., None]), 0.0)
    block_total = jnp.sum(weights, axis=-1)
    block_acc = jnp.einsum(
        "bkgp,bpkd->bkgd",
        weights.astype(jnp.bfloat16),
        value_cache,
        preferred_element_type=jnp.float32,
    )
    current_key = apply_rotary(new_key.astype(jnp.float32), query_pos[:, 0][:, None]).astype(
        jnp.bfloat16
    )
    self_score = (
        jnp.einsum(
            "lmzu,lmu->lmz", query_by_group[:, 0], current_key, preferred_element_type=jnp.float32
        )
        * scaling
    )
    fresh_values = new_value.astype(jnp.float32)[:, :, None, :]
    top_score = lax.pmax(jnp.maximum(block_max, self_score), "seq")
    factor = jnp.exp(block_max - top_score)
    summed_total, summed_acc = lax.psum(
        (block_total * factor, block_acc * factor[..., None]), "seq"
    )
    self_factor = jnp.exp(self_score - top_score)
    total = summed_total + self_factor
    accum = summed_acc + fresh_values * self_factor[..., None]
    attended = (
        (accum / total[..., None]).reshape(batch, heads_local * head_width).astype(jnp.bfloat16)
    )
    partial_value = jnp.dot(attended, out_weight, preferred_element_type=jnp.float32)
    return lax.psum(partial_value, "head")


def solution(mesh):
    placed = (
        P(None, "head", None),
        P(None, "seq", "head", None),
        P(None, "seq", "head", None),
        P(None, "head", None),
        P(None, "head", None),
        P(),
        P("head", "seq"),
    )
    return jax.shard_map(
        body, mesh=mesh, in_specs=placed, out_specs=P(None, "seq"), check_vma=False
    )
```

profile of v0, /device:TPU:0, one launch (start us, length us, event | category | flops | bytes accessed | tf_op | source)
XLA Modules:
  0.0 84.6 jit_solution(15212608247679977557)
XLA Ops:
  0.0 4.1 %copy_convert_fusion = f32[8,512,2,128]{3,1,2,0:T(8,128)} fusion(bf16[8,512,2,128]{3,2,1,0:T(2,128)(2,1)} %param.8), kind=kLoop, calls=%fused_computation.8 | loop fusion | flops 1048576 | bytes 6291456 | tf_op jit(solution)/shard_map/convert_element_type | solution.py:56
  4.1 1.0 %multiply_cosine_fusion = (f32[512,64]{1,0:T(8,128)S(1)}, f32[512,64]{1,0:T(8,128)S(1)}) fusion(f32[64]{0:T(128)S(1)} %multiply_exponential_fusion, f32[512]{0:T(512)S(1)} %get-tuple-element.35), kind=kLoop, calls=%fused_computation.13 | loop fusion | flops 32768 | bytes 264448 | tf_op jit(solution)/shard_map/cos | solution.py:18
  5.1 0.0 copy-start.4
  5.1 4.9 %subtract_convert_fusion = (bf16[8,512,2,64]{3,1,2,0:T(8,128)(2,1)S(1)}, bf16[8,512,2,64]{3,1,2,0:T(8,128)(2,1)S(1)}) fusion(f32[8,512,2,128]{3,1,2,0:T(8,128)} %copy_convert_fusion, f32[512,64]{1,0:T(8,128)S(1)} %get-tuple-element.27, f32[512,64]{1,0:T(8,128)S(1)} %get-tuple-element.26), kind=kLoop, calls=%fused_computation.1 | loop fusion | flops 4194304 | bytes 6553600 | tf_op jit(solution)/shard_map/convert.3
  10.1 0.1 pad.8.clone
  10.2 0.1 add_convert_fusion.3
  10.3 0.1 multiply_cosine_fusion.1
  10.4 0.1 fusion.46
  10.5 0.1 add_convert_fusion.1
  10.6 0.5 slice.45
  11.1 0.7 compare_bitcast_fusion.1
  11.8 0.1 broadcast_compare_fusion
  11.9 1.4 %fusion.47 = (f32[8,2,5]{2,1,0:T(2,128)S(1)}, f32[8,2,5,512]{3,2,1,0:T(8,128)S(1)}) fusion(bf16[8,512,2,64]{3,1,2,0:T(8,128)(2,1)S(1)} %get-tuple-element.17, bf16[8,512,2,64]{3,1,2,0:T(8,128)(2,1)S(1)} %get-tuple-element.16, bf16[8,3,2,5,64]{4,3,2,0,1:T(8,128)(2,1)S(1)} %get-tuple-element.19, bf16[8,3,2,5,64]{4,3,2,0,1:T(8,128)(2,1)S(1)} %get-tuple-element.18, ...), kind=kOutput, calls=%fused_computation.83 | convolution fusion | flops 14946224 | bytes 2326864 | tf_op jit(solution)/shard_map/bkgd,bpkd->bkgp/dot_general | solution.py:73
  13.3 0.2 fusion.15
  13.5 0.1 multiply_cosine_fusion.2
  13.6 0.1 subtract_convert_fusion.2
  13.7 0.1 maximum_bitcast_fusion
  13.8 0.2 fusion.33
  14.0 23.4 %pmax.7 = f32[8,2,5]{2,1,0:T(2,128)S(1)} all-reduce(f32[8,2,5]{2,1,0:T(2,128)S(1)} %multiply_maximum_fusion), channel_id=1, replica_groups=mesh['seq'=8,'head'=4] {'seq'}, use_global_device_ids=true, to_apply=%region_1.2 | all-reduce | flops 80 | bytes 640 | tf_op jit(solution)/shard_map/pmax | solution.py:96
  37.5 0.4 fusion.12
  37.9 33.9 %all-reduce = (f32[8,2,5,128]{3,2,1,0:T(8,128)S(1)}, f32[8,2,5]{2,1,0:T(2,128)S(1)}) all-reduce(f32[8,2,5,128]{3,2,1,0:T(8,128)S(1)} %fusion.12, f32[8,2,5]{2,1,0:T(2,128)S(1)} %bitcast.58), channel_id=1, replica_groups=mesh['seq'=8,'head'=4] {'seq'}, use_global_device_ids=true, to_apply=%region_2.3 | all-reduce | flops 10320 | bytes 82560 | tf_op jit(solution)/shard_map/psum | solution.py:98
  71.9 0.1 divide_convert_fusion
  72.0 1.8 %fusion.48 = f32[8,640]{1,0:T(8,128)S(1)} fusion(bf16[8,1280]{1,0:T(8,128)(2,1)S(1)} %convert_element_type.44, bf16[1280,640]{1,0:T(8,128)(2,1)} %param.13), kind=kOutput, calls=%fused_computation.84 | convolution fusion | flops 13107200 | bytes 1679360 | tf_op jit(solution)/shard_map/dot_general | solution.py:107
  73.8 10.9 %psum.23 = f32[8,640]{1,0:T(8,128)} all-reduce(f32[8,640]{1,0:T(8,128)S(1)} %fusion.48), channel_id=1, replica_groups=mesh['seq'=8,'head'=4] {'head'}, use_global_device_ids=true, to_apply=%region_5.6 | all-reduce | flops 5120 | bytes 40960 | tf_op jit(solution)/shard_map/psum | solution.py:108
  (25 shorter events, 0.2 us)
Async XLA Ops:
  0.0 37.5 %copy-start = (bf16[8,512,2,128]{3,2,1,0:T(2,128)(2,1)S(1)}, bf16[8,512,2,128]{3,2,1,0:T(2,128)(2,1)}, u32[]{:S(2)}) copy-start(bf16[8,512,2,128]{3,2,1,0:T(2,128)(2,1)} %param.9) | copy-start | bytes 6291460
  5.1 5.0 %copy-start.4 = (s32[8]{0:T(128)S(1)}, s32[8]{0:T(128)}, u32[]{:S(2)}) copy-start(s32[8]{0:T(128)} %param.12) | copy-start | bytes 100
  5.1 5.3 %copy-start.1 = (bf16[8,10,128]{2,0,1:T(8,128)(2,1)S(1)}, bf16[8,10,128]{2,0,1:T(8,128)(2,1)}, u32[]{:S(2)}) copy-start(bf16[8,10,128]{2,0,1:T(8,128)(2,1)} %param.7) | copy-start | bytes 61444
  11.9 1.6 %copy-start.2 = (bf16[8,2,128]{2,1,0:T(2,128)(2,1)S(1)}, bf16[8,2,128]{2,1,0:T(2,128)(2,1)}, u32[]{:S(2)}) copy-start(bf16[8,2,128]{2,1,0:T(2,128)(2,1)} %param.10) | copy-start | bytes 12292
  13.3 58.6 %copy-start.3 = (bf16[8,2,128]{2,1,0:T(2,128)(2,1)S(1)}, bf16[8,2,128]{2,1,0:T(2,128)(2,1)}, u32[]{:S(2)}) copy-start(bf16[8,2,128]{2,1,0:T(2,128)(2,1)} %param.11) | copy-start | bytes 12292
where the time goes:
time: 84.9 us; the launch traced here: 84.6 us
  blocking collectives  68.2 us (80%)
  other arithmetic  11.7 us (14%)
  matrix products  3.78 us (4%)
    psum x1, blocking collectives, body(): lax.psum((block_total * factor, block_acc * factor[..., None]), 'seq')  33.9 us
    pmax x1, blocking collectives, body(): top_score = lax.pmax(jnp.maximum(block_max, self_score), 'seq')  23.4 us
    psum x1, blocking collectives, body(): return lax.psum(partial_value, 'head')  10.9 us
    another operation x3, other arithmetic  5.08 us
    convert_element_type x1, other arithmetic, body(): key_cache.astype(jnp.float32)  4.08 us
    dot_general x1, matrix products, body(): jnp.dot(attended, out_weight, preferred_element_type=jnp.float32)  1.75 us

commit v1 on v0

--- a/solution.py
+++ b/solution.py
@@ -105,7 +105,7 @@
         (accum / total[..., None]).reshape(batch, heads_local * head_width).astype(jnp.bfloat16)
     )
     partial_value = jnp.dot(attended, out_weight, preferred_element_type=jnp.float32)
-    return lax.psum(partial_value, "head")
+    return jnp.sum(lax.all_gather(partial_value, "head"), axis=0)
 
 
 def solution(mesh):

time: 84.9 us -> 79.9 us (0.941)
  blocking collectives: 68.2 us -> 62.6 us
    psum x1 -> x0, blocking collectives: 10.9 us -> none  [body(): return lax.psum(partial_value, 'head')]
    all_gather x0 -> x1, blocking collectives: none -> 5.28 us  [body(): return jnp.sum(lax.all_gather(partial_value, 'head'), axis=0)]
where the time goes in v1:
time: 79.9 us; the launch traced here: 79.7 us
  blocking collectives  62.6 us (78%)
  other arithmetic  12.3 us (15%)
  matrix products  3.78 us (5%)
    psum x1, blocking collectives, body(): lax.psum((block_total * factor, block_acc * factor[..., None]), 'seq')  33.9 us
    pmax x1, blocking collectives, body(): top_score = lax.pmax(jnp.maximum(block_max, self_score), 'seq')  23.4 us
    all_gather x1, blocking collectives, body(): return jnp.sum(lax.all_gather(partial_value, 'head'), axis=0)  5.28 us
    another operation x3, other arithmetic  5.08 us
    convert_element_type x1, other arithmetic, body(): key_cache.astype(jnp.float32)  4.08 us
    dot_general x1, matrix products, body(): jnp.dot(attended, out_weight, preferred_element_type=jnp.float32)  1.75 us

profile of v1, /device:TPU:0, one launch (start us, length us, event | category | flops | bytes accessed | tf_op | source)
XLA Modules:
  0.0 79.7 jit_solution(10005468552995350053)
XLA Ops:
  0.0 4.1 %copy_convert_fusion = f32[8,512,2,128]{3,1,2,0:T(8,128)} fusion(bf16[8,512,2,128]{3,2,1,0:T(2,128)(2,1)} %param.8), kind=kLoop, calls=%fused_computation.8 | loop fusion | flops 1048576 | bytes 6291456 | tf_op jit(solution)/shard_map/convert_element_type | solution.py:56
  4.1 1.0 %multiply_cosine_fusion = (f32[512,64]{1,0:T(8,128)S(1)}, f32[512,64]{1,0:T(8,128)S(1)}) fusion(f32[64]{0:T(128)S(1)} %multiply_exponential_fusion, f32[512]{0:T(512)S(1)} %get-tuple-element.35), kind=kLoop, calls=%fused_computation.13 | loop fusion | flops 32768 | bytes 264448 | tf_op jit(solution)/shard_map/cos | solution.py:18
  5.1 4.9 %subtract_convert_fusion = (bf16[8,512,2,64]{3,1,2,0:T(8,128)(2,1)S(1)}, bf16[8,512,2,64]{3,1,2,0:T(8,128)(2,1)S(1)}) fusion(f32[8,512,2,128]{3,1,2,0:T(8,128)} %copy_convert_fusion, f32[512,64]{1,0:T(8,128)S(1)} %get-tuple-element.27, f32[512,64]{1,0:T(8,128)S(1)} %get-tuple-element.26), kind=kLoop, calls=%fused_computation.1 | loop fusion | flops 4194304 | bytes 6553600 | tf_op jit(solution)/shard_map/convert.3
  10.1 0.1 pad.8.clone
  10.2 0.1 add_convert_fusion.3
  10.3 0.1 multiply_cosine_fusion.1
  10.4 0.1 fusion.46
  10.5 0.1 add_convert_fusion.1
  10.6 0.5 slice.45
  11.1 0.7 compare_bitcast_fusion.1
  11.8 0.1 broadcast_compare_fusion
  11.9 1.4 %fusion.47 = (f32[8,2,5]{2,1,0:T(2,128)S(1)}, f32[8,2,5,512]{3,2,1,0:T(8,128)S(1)}) fusion(bf16[8,512,2,64]{3,1,2,0:T(8,128)(2,1)S(1)} %get-tuple-element.17, bf16[8,512,2,64]{3,1,2,0:T(8,128)(2,1)S(1)} %get-tuple-element.16, bf16[8,3,2,5,64]{4,3,2,0,1:T(8,128)(2,1)S(1)} %get-tuple-element.19, bf16[8,3,2,5,64]{4,3,2,0,1:T(8,128)(2,1)S(1)} %get-tuple-element.18, ...), kind=kOutput, calls=%fused_computation.84 | convolution fusion | flops 14946224 | bytes 2326864 | tf_op jit(solution)/shard_map/bkgd,bpkd->bkgp/dot_general | solution.py:73
  13.3 0.2 fusion.15
  13.5 0.1 multiply_cosine_fusion.2
  13.6 0.1 subtract_convert_fusion.2
  13.7 0.1 maximum_bitcast_fusion
  13.8 0.2 fusion.33
  14.0 23.4 %pmax.7 = f32[8,2,5]{2,1,0:T(2,128)S(1)} all-reduce(f32[8,2,5]{2,1,0:T(2,128)S(1)} %multiply_maximum_fusion), channel_id=1, replica_groups=mesh['seq'=8,'head'=4] {'seq'}, use_global_device_ids=true, to_apply=%region_1.2 | all-reduce | flops 80 | bytes 640 | tf_op jit(solution)/shard_map/pmax | solution.py:96
  37.5 0.4 fusion.12
  37.9 33.9 %all-reduce = (f32[8,2,5,128]{3,2,1,0:T(8,128)S(1)}, f32[8,2,5]{2,1,0:T(2,128)S(1)}) all-reduce(f32[8,2,5,128]{3,2,1,0:T(8,128)S(1)} %fusion.12, f32[8,2,5]{2,1,0:T(2,128)S(1)} %bitcast.60), channel_id=1, replica_groups=mesh['seq'=8,'head'=4] {'seq'}, use_global_device_ids=true, to_apply=%region_2.3 | all-reduce | flops 10320 | bytes 82560 | tf_op jit(solution)/shard_map/psum | solution.py:98
  71.9 0.1 divide_convert_fusion
  72.0 1.8 %fusion.48 = f32[8,640]{1,0:T(8,128)S(1)} fusion(bf16[8,1280]{1,0:T(8,128)(2,1)S(1)} %convert_element_type.44, bf16[1280,640]{1,0:T(8,128)(2,1)} %param.13), kind=kOutput, calls=%fused_computation.85 | convolution fusion | flops 13107200 | bytes 1679360 | tf_op jit(solution)/shard_map/dot_general | solution.py:107
  73.8 5.3 %all-gather = f32[32,640]{1,0:T(8,128)S(1)} all-gather(f32[8,640]{1,0:T(8,128)S(1)} %fusion.48), channel_id=2, replica_groups=mesh['seq'=8,'head'=4] {'head'}, dimensions={0}, use_global_device_ids=true | all-gather | bytes 102400 | tf_op jit(solution)/shard_map/all_gather | solution.py:108
  79.1 0.6 bitcast_reduce_fusion
  (26 shorter events, 0.2 us)
Async XLA Ops:
  0.0 37.5 %copy-start = (bf16[8,512,2,128]{3,2,1,0:T(2,128)(2,1)S(1)}, bf16[8,512,2,128]{3,2,1,0:T(2,128)(2,1)}, u32[]{:S(2)}) copy-start(bf16[8,512,2,128]{3,2,1,0:T(2,128)(2,1)} %param.9) | copy-start | bytes 6291460
  5.1 5.0 %copy-start.4 = (s32[8]{0:T(128)S(1)}, s32[8]{0:T(128)}, u32[]{:S(2)}) copy-start(s32[8]{0:T(128)} %param.12) | copy-start | bytes 100
  5.1 5.3 %copy-start.1 = (bf16[8,10,128]{2,0,1:T(8,128)(2,1)S(1)}, bf16[8,10,128]{2,0,1:T(8,128)(2,1)}, u32[]{:S(2)}) copy-start(bf16[8,10,128]{2,0,1:T(8,128)(2,1)} %param.7) | copy-start | bytes 61444
  11.9 1.6 %copy-start.2 = (bf16[8,2,128]{2,1,0:T(2,128)(2,1)S(1)}, bf16[8,2,128]{2,1,0:T(2,128)(2,1)}, u32[]{:S(2)}) copy-start(bf16[8,2,128]{2,1,0:T(2,128)(2,1)} %param.10) | copy-start | bytes 12292
  13.3 58.6 %copy-start.3 = (bf16[8,2,128]{2,1,0:T(2,128)(2,1)S(1)}, bf16[8,2,128]{2,1,0:T(2,128)(2,1)}, u32[]{:S(2)}) copy-start(bf16[8,2,128]{2,1,0:T(2,128)(2,1)} %param.11) | copy-start | bytes 12292
